TPU v7x, 32 devices: a whole 2x2x4 slice. The times are simulated.
32 devices in a mesh: face: 2 (over y), fy: 4 (over x, core), fx: 4 (over z).
Axes of the slice: x: 2, y: 2, z: 4, core: 2. Of those that a mesh axis runs over, the one named last changes fastest.
Arguments:
- state: float32 [6, 32, 32, 192], P('face', 'fy', 'fx'), may hold values from -6 to 6
- jacobian: float32 [6, 32, 32], P('face', 'fy', 'fx'), may hold values from 0.5 to 2
- metric_diag: float32 [2, 6, 32, 32], P(None, 'face', 'fy', 'fx'), may hold values from 0.6 to 1.4
- metric_cross: float32 [6, 32, 32], P('face', 'fy', 'fx'), may hold values from -0.3 to 0.3
- coriolis: float32 [6, 32, 32], P('face', 'fy', 'fx'), may hold values from -2 to 2
- nbr_face: int32 [6, 4], replicated, may hold values from 0 to 5, as said below
- nbr_edge: int32 [6, 4], replicated, may hold values from 0 to 3, as said below
Outputs:
- updated: float32 [6, 32, 32, 192], P('face', 'fy', 'fx')
Inputs may be any that keep to these rules, and one draw needn't show every extreme that they name: Edge e of a face is 0 south (row 0), 1 east (last column), 2 north (last row), 3 west (column 0). Edge e of face f is glued to edge nbr_edge[f, e] of face nbr_face[f, e], and that edge back to it; the 6 faces are glued as the surface of a cube, three faces at each corner, the two glued edges running in opposite senses when both are read counterclockwise. `nbr_edge`: see nbr_face.
All inputs are finite; a program needn't handle non-finite values.
Results may differ from a plain program's by a relative error of at most 0.0001.
Values sent between devices are 32-bit elements; how exact they have to be, the bound alone decides.
A program may use at most 64 MiB of HBM per device.

v0:
```python
import functools

import jax
import jax.numpy as jnp
import numpy as np
from jax import lax
from jax.experimental import pallas as pl
from jax.experimental.pallas import tpu as pltpu
from jax.sharding import PartitionSpec as P

time_step = 0.05
hyper_coeff = 0.0005
MESH = pl.DeviceIdType.MESH


def padded(cells, sides, width):
    for axis, dim in sides:
        count = lax.axis_size(axis)
        ends = count - 1
        head = lax.slice_in_dim(cells, 0, width, axis=dim)
        tail = lax.slice_in_dim(cells, cells.shape[dim] - width, cells.shape[dim], axis=dim)
        cells = jnp.concatenate(
            [
                lax.ppermute(tail, axis, [(i, (i + 1) % count) for i in range(ends)]),
                cells,
                lax.ppermute(head, axis, [((i + 1) % count, i) for i in range(ends)]),
            ],
            axis=dim,
        )
    return cells


def deriv_table():
    gll_nodes = np.array([-1.0, -1.0 / np.sqrt(5.0), 1.0 / np.sqrt(5.0), 1.0])
    bary_weights = np.ones(4)
    for j in range(4):
        for m in range(4):
            if m != j:
                bary_weights[j] = bary_weights[j] / (gll_nodes[j] - gll_nodes[m])
    matrix = np.zeros((4, 4))
    for i in range(4):
        for j in range(4):
            if i != j:
                matrix[i, j] = bary_weights[j] / bary_weights[i] / (gll_nodes[i] - gll_nodes[j])
        matrix[i, i] = -np.sum(matrix[i])
    return matrix


def along_x(values):
    face_count, row_count, col_count, chan_count = values.shape
    blocks = values.reshape(face_count, row_count, col_count // 4, 4, chan_count)
    result = jnp.einsum(
        "jk,abekc->abejc",
        jnp.asarray(deriv_table(), jnp.float32),
        blocks,
        precision=lax.Precision.HIGHEST,
    )
    return result.reshape(values.shape)


def along_y(values):
    face_count, row_count, col_count, chan_count = values.shape
    blocks = values.reshape(face_count, row_count // 4, 4, col_count, chan_count)
    result = jnp.einsum(
        "ik,aekxc->aeixc",
        jnp.asarray(deriv_table(), jnp.float32),
        blocks,
        precision=lax.Precision.HIGHEST,
    )
    return result.reshape(values.shape)


def mass_of(jacobian):
    weights = jnp.asarray([1.0 / 6.0, 5.0 / 6.0, 5.0 / 6.0, 1.0 / 6.0], jnp.float32)
    row_weight = jnp.tile(weights, jacobian.shape[1] // 4)
    col_weight = jnp.tile(weights, jacobian.shape[2] // 4)
    return jacobian * row_weight[None, :, None] * col_weight[None, None, :]


def tendency(state, geometry, planet):
    volume, metric_xx, metric_yy, metric_xy = geometry
    levels = state.shape[-1] // 3
    wind_u = state[..., :levels]
    wind_v = state[..., levels : 2 * levels]
    temper = state[..., 2 * levels :]
    contra_u = metric_xx * wind_u + metric_xy * wind_v
    contra_v = metric_xy * wind_u + metric_yy * wind_v
    energy = 0.5 * (wind_u * contra_u + wind_v * contra_v) + temper
    xderivs = along_x(jnp.concatenate([wind_v, temper, energy], -1))
    yderivs = along_y(jnp.concatenate([wind_u, temper, energy], -1))
    absolute = (xderivs[..., :levels] - yderivs[..., :levels]) / volume + planet
    tend_u = absolute * volume * contra_v - xderivs[..., 2 * levels :]
    tend_v = -absolute * volume * contra_u - yderivs[..., 2 * levels :]
    tend_t = -(
        contra_u * xderivs[..., levels : 2 * levels] + contra_v * yderivs[..., levels : 2 * levels]
    )
    return state + time_step * jnp.concatenate([tend_u, tend_v, tend_t], -1)


def laplace(values, geometry):
    volume, metric_xx, metric_yy, metric_xy = geometry
    grad_x = along_x(values)
    grad_y = along_y(values)
    flux_x = volume * (metric_xx * grad_x + metric_xy * grad_y)
    flux_y = volume * (metric_xy * grad_x + metric_yy * grad_y)
    return (along_x(flux_x) + along_y(flux_y)) / volume


def combine(values, axis):
    length = values.shape[axis] - 2
    positions = jnp.arange(length)
    leading = (positions % 4 == 0).astype(jnp.float32)
    trailing = (positions % 4 == 3).astype(jnp.float32)
    broad_shape = [1, 1, 1, 1]
    broad_shape[axis] = length
    leading = leading.reshape(broad_shape)
    trailing = trailing.reshape(broad_shape)
    middle = lax.slice_in_dim(values, 1, length + 1, axis=axis)
    previous = lax.slice_in_dim(values, 0, length, axis=axis)
    following = lax.slice_in_dim(values, 2, length + 2, axis=axis)
    return middle + leading * previous + trailing * following


def rotate(segment, quarter, levels):
    cosine = ((quarter == 0).astype(jnp.float32) - (quarter == 2).astype(jnp.float32))[..., None]
    sine_part = ((quarter == 1).astype(jnp.float32) - (quarter == 3).astype(jnp.float32))[..., None]
    wind_u = segment[..., :levels]
    wind_v = segment[..., levels : 2 * levels]
    return jnp.concatenate(
        [
            cosine * wind_u - sine_part * wind_v,
            sine_part * wind_u + cosine * wind_v,
            segment[..., 2 * levels :],
        ],
        -1,
    )


def in_face(values):
    across = combine(padded(values, (("fx", 2),), 1), 2)
    return combine(padded(across, (("fy", 1),), 1), 1)


def place_pieces(
    got_flat,
    got_tall,
    vector,
    nbr_edge,
    flat_edge,
    tall_edge,
    on_south,
    on_west,
    flat_start,
    tall_start,
    face_local,
    side_nodes,
    chan_count,
    levels,
):
    edge_ids = jnp.arange(4, dtype=jnp.int32)
    flat_target = nbr_edge[:, flat_edge]
    tall_target = nbr_edge[:, tall_edge]
    if vector:
        got_flat = rotate(got_flat, ((flat_target - flat_edge + 2) % 4)[None, :, None], levels)
        got_tall = rotate(got_tall, ((tall_target - tall_edge + 2) % 4)[None, :, None], levels)
    got_flat = jnp.where(on_south, got_flat[:, :, ::-1], got_flat)
    got_tall = jnp.where(on_west, got_tall, got_tall[:, :, ::-1])
    flat_pick = (flat_target[:, None] == edge_ids[None, :]).astype(jnp.float32)
    tall_pick = (tall_target[:, None] == edge_ids[None, :]).astype(jnp.float32)
    flat_rims = jnp.einsum("se,gsjc->gejc", flat_pick, got_flat, precision=lax.Precision.HIGHEST)
    tall_rims = jnp.einsum("se,gsjc->gejc", tall_pick, got_tall, precision=lax.Precision.HIGHEST)
    empty_rims = jnp.zeros((face_local, 4, side_nodes, chan_count), jnp.float32)
    rim_strips = lax.dynamic_update_slice(empty_rims, flat_rims, (0, 0, flat_start, 0))
    return rim_strips + lax.dynamic_update_slice(empty_rims, tall_rims, (0, 0, tall_start, 0))


def outgoing(
    summed, nbr_face, face_ids, flat_edge, tall_edge, on_south, on_west, flat_live, tall_live
):
    row_count = summed.shape[1]
    col_count = summed.shape[2]
    all_faces = jnp.arange(nbr_face.shape[0], dtype=jnp.int32)
    flat_piece = jnp.where(on_south, summed[:, 0], summed[:, row_count - 1])
    tall_piece = jnp.where(on_west, summed[:, :, 0], summed[:, :, col_count - 1])
    flat_dest = nbr_face[face_ids, flat_edge]
    tall_dest = nbr_face[face_ids, tall_edge]
    flat_send = ((all_faces[:, None] == flat_dest[None, :]) & flat_live).astype(jnp.float32)
    tall_send = ((all_faces[:, None] == tall_dest[None, :]) & tall_live).astype(jnp.float32)
    return (
        flat_send[:, :, None, None] * flat_piece[None],
        tall_send[:, :, None, None] * tall_piece[None],
    )


def assemble(values, vector, nbr_face, nbr_edge):
    summed = in_face(values)
    face_local, row_count, col_count, chan_count = summed.shape
    levels = chan_count // 3
    row_index = lax.axis_index("fy")
    col_index = lax.axis_index("fx")
    side_nodes = row_count * lax.axis_size("fy")
    face_ids = lax.axis_index("face") * face_local + jnp.arange(face_local, dtype=jnp.int32)
    on_south = row_index == 0
    on_north = row_index == lax.axis_size("fy") - 1
    on_west = col_index == 0
    on_east = col_index == lax.axis_size("fx") - 1
    flat_live = on_south | on_north
    tall_live = on_west | on_east
    flat_edge = jnp.where(on_south, 0, 2).astype(jnp.int32)
    tall_edge = jnp.where(on_west, 3, 1).astype(jnp.int32)
    flat_start = jnp.where(
        on_south, side_nodes - (col_index + 1) * col_count, col_index * col_count
    )
    tall_start = jnp.where(on_west, row_index * row_count, side_nodes - (row_index + 1) * row_count)
    send_flat, send_tall = outgoing(
        summed, nbr_face, face_ids, flat_edge, tall_edge, on_south, on_west, flat_live, tall_live
    )
    got_flat, got_tall = (
        lax.all_to_all(send_flat, "face", split_axis=0, concat_axis=1, tiled=True),
        lax.all_to_all(send_tall, "face", split_axis=0, concat_axis=1, tiled=True),
    )
    rim_strips = place_pieces(
        got_flat,
        got_tall,
        vector,
        nbr_edge,
        flat_edge,
        tall_edge,
        on_south,
        on_west,
        flat_start,
        tall_start,
        face_local,
        side_nodes,
        chan_count,
        levels,
    )
    flat_lines = jnp.stack([rim_strips[:, 0], rim_strips[:, 2, ::-1]], axis=1)
    flat_lines = flat_lines.reshape(face_local, 2, lax.axis_size("fx"), col_count, chan_count)
    tall_lines = jnp.stack([rim_strips[:, 1], rim_strips[:, 3, ::-1]], axis=1)
    tall_lines = tall_lines.reshape(face_local, 2, lax.axis_size("fy"), row_count, chan_count)
    flat_whole = lax.psum(flat_lines, "fy")
    tall_whole = lax.psum(tall_lines, "fx")
    flat_block = lax.psum_scatter(flat_whole, "fx", scatter_dimension=2, tiled=True)
    tall_block = lax.psum_scatter(tall_whole, "fy", scatter_dimension=2, tiled=True)
    flat_add = jnp.where(on_south, flat_block[:, 0, 0], flat_block[:, 1, 0])
    tall_add = jnp.where(on_west, tall_block[:, 1, 0], tall_block[:, 0, 0])
    result = summed.at[:, 0].add(jnp.where(on_south, flat_add, 0.0))
    result = result.at[:, row_count - 1].add(jnp.where(on_north, flat_add, 0.0))
    result = result.at[:, :, 0].add(jnp.where(on_west, tall_add, 0.0))
    result = result.at[:, :, col_count - 1].add(jnp.where(on_east, tall_add, 0.0))
    return result


def per_device(state, jacobian, metric_diag, metric_cross, coriolis, nbr_face, nbr_edge):
    node_mass = mass_of(jacobian)[..., None]
    total_mass = assemble(node_mass, False, nbr_face, nbr_edge)
    geometry = (
        jacobian[..., None],
        metric_diag[0][..., None],
        metric_diag[1][..., None],
        metric_cross[..., None],
    )
    raw = tendency(state, geometry, coriolis[..., None])
    sectioned = assemble(node_mass * raw, True, nbr_face, nbr_edge) / total_mass
    first_lap = (
        assemble(node_mass * laplace(sectioned, geometry), True, nbr_face, nbr_edge) / total_mass
    )
    second_lap = (
        assemble(node_mass * laplace(first_lap, geometry), True, nbr_face, nbr_edge) / total_mass
    )
    return sectioned - hyper_coeff * second_lap


SIDE = 8
HALF = 64
LANES = 128


def widen(ref, index, r):
    row = jnp.broadcast_to(ref[index + (pl.ds(r, 1), slice(None))].reshape(1, SIDE), (SIDE, SIDE))
    eye = lax.broadcasted_iota(jnp.int32, (SIDE, SIDE), 0) == lax.broadcasted_iota(jnp.int32, (SIDE, SIDE), 1)
    return jnp.broadcast_to(jnp.sum(jnp.where(eye, row, 0.0), axis=1, keepdims=True), (SIDE, LANES))


def up(v, count, axis):
    return pltpu.roll(v, v.shape[axis] - count, axis)


def down(v, count, axis):
    return pltpu.roll(v, count, axis)


def slope(a):
    d = deriv_table()
    p0, p1, m0, m1 = a[0] + a[3], a[1] + a[2], a[0] - a[3], a[1] - a[2]
    bend = p0 - p1
    o0 = jnp.float32((d[0, 0] + d[0, 3]) / 2) * bend
    o1 = jnp.float32((d[1, 0] + d[1, 3]) / 2) * bend
    q0 = jnp.float32((d[0, 0] - d[0, 3]) / 2) * m0 + jnp.float32((d[0, 1] - d[0, 2]) / 2) * m1
    q1 = jnp.float32((d[1, 0] - d[1, 3]) / 2) * m0 + jnp.float32((d[1, 1] - d[1, 2]) / 2) * m1
    return [q0 + o0, q1 + o1, q1 - o1, q0 - o0]


def slope_x(v):
    return [slope(v[i]) for i in range(4)]


def slope_y(v):
    cols = [slope([v[i][j] for i in range(4)]) for j in range(4)]
    return [[cols[j][i] for j in range(4)] for i in range(4)]


def element_rows(mix, er, i, which):
    start = er * 64 + which * 16 + i * 4
    return mix.at[pl.ds(start, 4)], mix.at[pl.ds(start + 32, 4)]


def spread(mix, plane, er, i, which, v):
    for ec in range(2):
        mix[plane, pl.ds(er * 64 + ec * 32 + which * 16 + i * 4, 4), :] = v[4 * ec : 4 * ec + 4]


def by_node(mix, plane):
    return jnp.concatenate([mix[plane, pl.ds(n, 8, stride=16), :] for n in range(16)], axis=0)


def main_kernel(
    groups,
    blocks,
    nbr_face,
    nbr_edge,
    state,
    jac,
    diag,
    cross,
    coriolis,
    out,
    mix,
    send,
    send_geo,
    got,
    got_geo,
    coef,
    section,
    back,
    sem_s_geo,
    sem_r_geo,
    sem_s_in,
    sem_r_in,
    sem_s_out,
    sem_r_out,
    sem_own,
):
    faces = state.shape[0]
    count = groups * blocks * blocks
    last = blocks - 1
    g = lax.axis_index("face")
    y = lax.axis_index("fy")
    x = lax.axis_index("fx")
    me = (g * blocks + y) * blocks + x

    def others():
        for dx in (2, 3, 1, 0):
            for dy in range(blocks):
                for dg in range(groups):
                    if dx or dy or dg:
                        at = (lax.rem(g + dg, groups), lax.rem(y + dy, blocks), lax.rem(x + dx, blocks))
                        yield (at[0] * blocks + at[1]) * blocks + at[2], at

    barrier = pltpu.get_barrier_semaphore()
    for _, at in others():
        pl.semaphore_signal(barrier, inc=1, device_id=at, device_id_type=MESH)

    sub = lax.broadcasted_iota(jnp.int32, (SIDE, LANES), 0)
    lane = lax.broadcasted_iota(jnp.int32, (SIDE, LANES), 1)
    low = lane < HALF
    node = sub % 4
    table = deriv_table()
    weights = (1.0 / 6.0, 5.0 / 6.0, 5.0 / 6.0, 1.0 / 6.0)
    zero = jnp.zeros((SIDE, LANES), jnp.float32)

    def per_node(entries):
        total = jnp.full((SIDE, LANES), entries[0], jnp.float32)
        for j in range(1, 4):
            total = jnp.where(node == j, jnp.float32(entries[j]), total)
        return total

    col_weight = per_node(weights)
    taps = {
        s: per_node([float(table[j, j + s]) if 0 <= j + s < 4 else 0.0 for j in range(4)])
        for s in range(-3, 4)
    }

    def swap(v):
        return pltpu.roll(v, HALF, 1)

    def along_sub(v):
        total = taps[0] * v
        for s in (-3, -2, -1, 1, 2, 3):
            total = total + taps[s] * pltpu.roll(v, (-s) % SIDE, 0)
        return total

    second = (lane >= 32) & (lane < 64)
    geo = [[[None, None] for _ in range(SIDE)] for _ in range(faces)]
    for f in range(faces):
        for start in range(0, SIDE, 4):
            wind, temp, contra, energy, vol, cor, mass = [], [], [], [], [], [], []
            for r in range(start, start + 4):
                j = widen(jac, (f,), r)
                m_xx, m_yy, m_xy = widen(diag, (0, f), r), widen(diag, (1, f), r), widen(cross, (f,), r)
                w = state[f, r, :, 0 : 2 * HALF]
                t = state[f, r, :, 2 * HALF : 3 * HALF]
                t = jnp.concatenate([t, t], axis=1)
                c = jnp.where(low, m_xx, m_yy) * w + m_xy * swap(w)
                p = w * c
                wind.append(w)
                temp.append(t)
                contra.append(c)
                energy.append(0.5 * (p + swap(p)) + t)
                vol.append(j)
                cor.append(widen(coriolis, (f,), r))
                mass.append(j * (jnp.float32(weights[r % 4]) * col_weight))
                even = lane % 2 == 0
                geo[f][r][0] = jnp.where(even, j * m_xx, j * m_yy)
                geo[f][r][1] = jnp.where(even, j * m_xy, mass[-1])
            dxs = [along_sub(jnp.where(low, energy[i], wind[i])) for i in range(4)]
            dys = slope([jnp.where(low, wind[i], energy[i]) for i in range(4)])
            dxt = [along_sub(temp[i]) for i in range(4)]
            dyt = slope(temp)
            for i in range(4):
                dxv = jnp.where(low, swap(dxs[i]), dxs[i])
                dyu = jnp.where(low, dys[i], swap(dys[i]))
                spin = (dxv - dyu) + cor[i] * vol[i]
                spin = jnp.where(low, spin, -spin)
                tend = spin * swap(contra[i]) - jnp.where(low, dxs[i], dys[i])
                fresh = mass[i] * (wind[i] + time_step * tend)
                q = contra[i] * jnp.where(low, dxt[i], dyt[i])
                heat = mass[i] * (temp[i] - time_step * (q + swap(q)))
                er = start // 4
                spread(mix, f, er, i, 0, jnp.where(second, down(heat, 32, 1), fresh))
                spread(mix, f, er, i, 1, jnp.where(second, heat, up(fresh, 32, 1)))
    for r in range(SIDE):
        for h in range(2):
            v = geo[0][r][h]
            for f in range(1, faces):
                v = jnp.where(lane >= 2 * f, geo[f][r][h], v)
            spread(mix, faces, r // 4, r % 4, h, v)
    for f in range(faces):
        turned = by_node(mix, f).T
        for k, part in enumerate((0, 2, 1)):
            send[k * faces + f] = turned[part * count : (part + 1) * count]
    send_geo[...] = by_node(mix, faces).T[0:SIDE]

    er, ec, lev = sub // 4, (sub // 2) % 2, sub % 2
    lx, ly = lane % blocks, (lane // blocks) % blocks
    panel = lane // (blocks * blocks)
    er0, er1, ec0, ec1 = er == 0, er == 1, ec == 0, ec == 1
    x_lo, x_hi, y_lo, y_hi = lx == 0, lx == last, ly == 0, ly == last
    edge_at = (er0 & y_lo, er1 & x_hi, er0 & y_hi, er1 & x_lo)

    first_at = jnp.zeros((SIDE, LANES), jnp.int32)
    step_at, quarter_at = first_at, first_at
    for e in range(4):
        firsts, steps, quarters = first_at * 0, first_at * 0, first_at * 0
        for f in range(faces):
            for k in range(groups):
                nf = nbr_face[e, k * faces + f]
                ne = nbr_edge[e, k * faces + f]
                nl, ng = nf % faces, nf // faces
                tall = ne % 2
                step = 1 + tall * (blocks - 1)
                flips = jnp.where(ne >= 2, 0 if e < 2 else 1, 1 if e < 2 else 0)
                offset = jnp.where(ne == 2, last * blocks, jnp.where(ne == 1, last, 0))
                first = (nl * groups + ng) * (blocks * blocks) + offset + flips * (last * step)
                here = panel == f * groups + k
                firsts = jnp.where(here, first, firsts)
                steps = jnp.where(here, step * (1 - 2 * flips), steps)
                quarters = jnp.where(here, (e - ne + 2 + 4) % 4, quarters)
        first_at = jnp.where(edge_at[e], firsts, first_at)
        step_at = jnp.where(edge_at[e], steps, step_at)
        quarter_at = jnp.where(edge_at[e], quarters, quarter_at)
    source_at = first_at + step_at * jnp.where(er0, lx, ly)
    flipped = step_at < 0
    from_flat = (step_at == 1) | (step_at == -1)
    cosine = jnp.where(quarter_at == 0, 1.0, jnp.where(quarter_at == 2, -1.0, 0.0))
    sine = jnp.where(quarter_at == 1, 1.0, jnp.where(quarter_at == 3, -1.0, 0.0))

    def next_row(v):
        s = down(v, 4, 0)
        return jnp.where(er0, s, jnp.where(y_hi, zero, up(s, blocks, 1)))

    def prev_row(v):
        s = down(v, 4, 0)
        return jnp.where(er1, s, jnp.where(y_lo, zero, down(s, blocks, 1)))

    def next_col(v):
        return jnp.where(ec0, up(v, 2, 0), jnp.where(x_hi, zero, up(down(v, 2, 0), 1, 1)))

    def prev_col(v):
        return jnp.where(ec1, down(v, 2, 0), jnp.where(x_lo, zero, down(up(v, 2, 0), 1, 1)))

    def within(v):
        v = [list(row) for row in v]
        for j in range(4):
            a, b = v[0][j], v[3][j]
            v[0][j], v[3][j] = a + prev_row(b), b + next_row(a)
        for i in range(4):
            a, b = v[i][0], v[i][3]
            v[i][0], v[i][3] = a + prev_col(b), b + next_col(a)
        return v

    def rims(v):
        found = []
        for b in range(4):
            flat = jnp.where(y_hi, v[3][b], v[0][b])
            flat = jnp.where(er0 == y_hi, down(flat, 4, 0), flat)
            tall = jnp.where(x_hi, v[b][3], v[b][0])
            tall = jnp.where(ec0 == x_hi, jnp.where(x_hi, up(tall, 2, 0), down(tall, 2, 0)), tall)
            tall = jnp.where(er == ec, tall, down(tall, 4, 0))
            flat = jnp.take_along_axis(flat, source_at, axis=1, mode="promise_in_bounds")
            tall = jnp.take_along_axis(tall, source_at, axis=1, mode="promise_in_bounds")
            found.append(jnp.where(from_flat, flat, tall))
        partner = []
        for b in range(4):
            w = found[3 - b]
            w = jnp.where(ec0, up(w, 2, 0), down(w, 2, 0))
            partner.append(jnp.where(flipped, w, found[b]))
        return partner

    def add_rims(v, partner):
        for b in range(4):
            p = partner[b]
            s = down(p, 4, 0)
            v[0][b] = v[0][b] + jnp.where(edge_at[0], p, zero)
            v[3][b] = v[3][b] + jnp.where(er1 & y_hi, s, zero)
            q = jnp.where(er1, p, s)
            q = jnp.where(er == ec, q, jnp.where(er0, down(q, 2, 0), up(q, 2, 0)))
            v[b][0] = v[b][0] + jnp.where(ec0 & x_lo, q, zero)
            v[b][3] = v[b][3] + jnp.where(ec1 & x_hi, q, zero)
        return v

    def assemble_one(v):
        v = within(v)
        return add_rims(v, rims(v))

    def assemble_pair(u, v):
        u, v = within(u), within(v)
        pu, pv = rims(u), rims(v)
        tu = [cosine * a - sine * b for a, b in zip(pu, pv)]
        tv = [sine * a + cosine * b for a, b in zip(pu, pv)]
        return add_rims(u, tu), add_rims(v, tv)

    def grid(flat):
        return [[flat[8 * (4 * i + j) : 8 * (4 * i + j) + 8] for j in range(4)] for i in range(4)]

    def receive(ref, planes):
        blocks_in = [ref[p] for p in planes]
        blocks_in += [blocks_in[0]] * (LANES // count - len(blocks_in))
        return grid(jnp.concatenate(blocks_in, axis=0).T)

    def put(ref, k, v):
        for i in range(4):
            for j in range(4):
                ref[k, i, j] = v[i][j]

    def take(ref, k):
        return [[ref[k, i, j] for j in range(4)] for i in range(4)]

    def each(fn, *vs):
        return [[fn(*(v[i][j] for v in vs)) for j in range(4)] for i in range(4)]

    def copies(src_of, dst, sem_s, sem_r):
        for d, at in others():
            pltpu.make_async_remote_copy(
                src_ref=src_of(d),
                dst_ref=dst,
                send_sem=sem_s,
                recv_sem=sem_r,
                device_id=at,
                device_id_type=MESH,
            ).start()

    def all_of(ref, sem_s, sem_r):
        part = ref.at[:, pl.ds(0, count - 1)]
        return pltpu.make_async_remote_copy(
            src_ref=part,
            dst_ref=part,
            send_sem=sem_s,
            recv_sem=sem_r,
            device_id=(g, y, lax.rem(x + 1, blocks)),
            device_id_type=MESH,
        )

    pairs = 2 * faces
    pl.semaphore_wait(barrier, count - 1)
    copies(lambda d: send_geo.at[pl.ds(0, pairs)], got_geo.at[:, me], sem_s_geo, sem_r_geo)
    copies(lambda d: send.at[:, d], got.at[:, me], sem_s_in, sem_r_in)
    for q in range(pairs):
        got_geo[q, pl.ds(me, 1), :] = send_geo[pl.ds(q, 1), :]
    for q in range(3 * faces):
        got[q, pl.ds(me, 1), :] = send[q, pl.ds(me, 1), :]

    all_of(got_geo, sem_s_geo, sem_r_geo).wait_recv()
    for p in range(2):
        both = receive(got_geo, range(p, pairs, 2))
        put(coef, 2 * p, each(lambda v: jnp.where(lev == 0, v, down(v, 1, 0)), both))
        put(coef, 2 * p + 1, each(lambda v: jnp.where(lev == 1, v, up(v, 1, 0)), both))
    put(coef, 3, each(lambda v: 1.0 / v, assemble_one(take(coef, 3))))

    def fields_in(k):
        return receive(got, range(k * faces, (k + 1) * faces))

    def scaled(v):
        return each(lambda a, b: a * b, v, take(coef, 3))

    def laplace_of(v):
        a, b, c = take(coef, 0), take(coef, 1), take(coef, 2)
        gx, gy = slope_x(v), slope_y(v)
        fx = each(lambda p, q, m, n: m * p + n * q, gx, gy, a, b)
        fy = each(lambda p, q, m, n: m * p + n * q, gx, gy, b, c)
        total = each(lambda p, q: p + q, slope_x(fx), slope_y(fy))
        return [[jnp.float32(weights[i] * weights[j]) * total[i][j] for j in range(4)] for i in range(4)]

    def finish(k, v):
        done = each(lambda s, a: s - hyper_coeff * a, take(section, k), v)
        turned = jnp.concatenate([done[i][j] for i in range(4) for j in range(4)], axis=0).T
        for f in range(faces):
            back[k * faces + f] = turned[f * count : (f + 1) * count]

    def send_back(k, n):
        part = pl.ds(k * faces, n * faces)
        copies(lambda d: back.at[part, d], out.at[part, me], sem_s_out, sem_r_out)
        own = pltpu.make_async_copy(back.at[part, me], out.at[part, me], sem_own.at[k])
        own.start()
        return own

    all_of(got, sem_s_in, sem_r_in).wait_recv()
    heat = scaled(assemble_one(fields_in(2)))
    put(section, 2, heat)
    wind_u, wind_v = assemble_pair(fields_in(0), fields_in(1))
    put(section, 0, scaled(wind_u))
    put(section, 1, scaled(wind_v))
    heat = scaled(assemble_one(laplace_of(heat)))
    heat = scaled(assemble_one(laplace_of(heat)))
    finish(2, heat)
    own_t = send_back(2, 1)
    wind_u, wind_v = assemble_pair(laplace_of(take(section, 0)), laplace_of(take(section, 1)))
    wind_u, wind_v = assemble_pair(laplace_of(scaled(wind_u)), laplace_of(scaled(wind_v)))
    finish(0, scaled(wind_u))
    finish(1, scaled(wind_v))
    own_w = send_back(0, 2)
    all_of(got_geo, sem_s_geo, sem_r_geo).wait_send()
    all_of(got, sem_s_in, sem_r_in).wait_send()
    own_t.wait()
    own_w.wait()
    all_of(out, sem_s_out, sem_r_out).wait_send()
    all_of(out, sem_s_out, sem_r_out).wait_recv()


def last_kernel(got, out, mix):
    faces = out.shape[0]
    lane = lax.broadcasted_iota(jnp.int32, (SIDE, LANES), 1)
    even = (lane // 32) % 2 == 0
    for f in range(faces):
        u, v, t = (got[k * faces + f] for k in range(3))
        turned = jnp.concatenate([u, t, v, v], axis=0).T
        for n in range(16):
            mix[f, pl.ds(n, 8, stride=16), :] = turned[8 * n : 8 * n + 8]
        for r in range(SIDE):
            start = (r // 4) * 64 + (r % 4) * 4
            a, b = (
                jnp.concatenate([mix[f, pl.ds(start + h * 16 + ec * 32, 4), :] for ec in range(2)], axis=0)
                for h in range(2)
            )
            out[f, r, :, 0 : 2 * HALF] = jnp.where(even, a, down(b, 32, 1))
            out[f, r, :, 2 * HALF : 3 * HALF] = jnp.where(even, up(a, 32, 1), b)[:, 0:HALF]


def by_level(groups, blocks, state, jacobian, metric_diag, metric_cross, coriolis, nbr_face, nbr_edge):
    faces = state.shape[0]
    count = groups * blocks * blocks
    vmem, smem = pl.BlockSpec(memory_space=pltpu.VMEM), pl.BlockSpec(memory_space=pltpu.SMEM)
    piece = (3 * faces, count, LANES)
    cells = (4, 4, SIDE, LANES)
    dma = pltpu.SemaphoreType.DMA
    got = pl.pallas_call(
        functools.partial(main_kernel, groups, blocks),
        out_shape=jax.ShapeDtypeStruct(piece, jnp.float32),
        in_specs=[smem, smem] + [vmem] * 5,
        out_specs=pl.BlockSpec(memory_space=pltpu.HBM),
        scratch_shapes=[
            pltpu.VMEM((faces + 1, LANES, LANES), jnp.float32),
            pltpu.VMEM(piece, jnp.float32),
            pltpu.VMEM((SIDE, LANES), jnp.float32),
            pltpu.VMEM(piece, jnp.float32),
            pltpu.VMEM((2 * faces, count, LANES), jnp.float32),
            pltpu.VMEM((4,) + cells, jnp.float32),
            pltpu.VMEM((3,) + cells, jnp.float32),
            pltpu.VMEM(piece, jnp.float32),
        ]
        + [dma] * 6
        + [dma((3,))],
        compiler_params=pltpu.CompilerParams(collective_id=0, has_side_effects=True),
    )(nbr_face.T, nbr_edge.T, state, jacobian, metric_diag, metric_cross, coriolis)
    return pl.pallas_call(
        last_kernel,
        out_shape=jax.ShapeDtypeStruct(state.shape, jnp.float32),
        in_specs=[vmem],
        out_specs=vmem,
        scratch_shapes=[pltpu.VMEM((faces, LANES, LANES), jnp.float32)],
    )(got)


def solution(mesh):
    groups, rows, columns = (mesh.shape[axis] for axis in ("face", "fy", "fx"))
    count = groups * rows * columns

    def body(*args):
        state = args[0]
        faces = state.shape[0]
        fits = rows == columns == 4 and 2 * count == HALF and faces * count <= LANES
        if fits and state.shape[1:] == (SIDE, SIDE, 3 * HALF) and 2 * faces <= SIDE:
            return by_level(groups, rows, *args)
        return per_device(*args)

    return jax.shard_map(
        body,
        mesh=mesh,
        in_specs=(
            P("face", "fy", "fx", None),
            P("face", "fy", "fx"),
            P(None, "face", "fy", "fx"),
            P("face", "fy", "fx"),
            P("face", "fy", "fx"),
            P(),
            P(),
        ),
        out_specs=P("face", "fy", "fx", None),
        check_vma=False,
    )
```

profile of v0, /device:TPU:0, one launch (start us, length us, event | category | flops | bytes accessed | tf_op | source)
XLA Modules:
  0.0 25.2 jit_solution(1519879861598141809)
XLA Ops:
  0.0 23.3 %shard_map.73.got = f32[9,32,128]{2,1,0:T(8,128)} custom-call(s32[4,6]{1,0:T(4,128)} %bitcast.2, s32[4,6]{1,0:T(4,128)} %bitcast.3, f32[3,8,8,192]{3,2,1,0:T(8,128)} %state.1, f32[3,8,8]{2,1,0:T(8,128)} %jac.1, f32[2,3,8,8]{3,2,1,0:T(8,128)} %diag.1, f32[3,8,8]{2,1,0:T(8,128)} %cross.1, f32[3,8,8]{2,1,0:T(8,128)} %coriolis.1), custom_call_target="tpu_custom_call" | custom-call | tf_op jit(solution)/shard_map/pallas_call | solution.py:687
  23.4 1.8 %shard_map.74 = f32[3,8,8,192]{3,2,1,0:T(8,128)} custom-call(f32[9,32,128]{2,1,0:T(8,128)} %shard_map.73.got), custom_call_target="tpu_custom_call" | custom-call | tf_op jit(solution)/shard_map/pallas_call | solution.py:706
where the time goes:
time: 25.4 us; the launch traced here: 25.2 us
  Pallas kernels  25.2 us (99%)
    pallas_call x1, Pallas kernels, by_level(): pl.pallas_call(functools.partial(main_kernel, groups, blocks), out_shape=...  23.3 us
    pallas_call x1, Pallas kernels, by_level(): pl.pallas_call(last_kernel, out_shape=jax.ShapeDtypeStruct(state.shape, j...  1.83 us

commit v1 on v0

--- a/solution.py
+++ b/solution.py
@@ -277,12 +277,6 @@
 LANES = 128
 
 
-def widen(ref, index, r):
-    row = jnp.broadcast_to(ref[index + (pl.ds(r, 1), slice(None))].reshape(1, SIDE), (SIDE, SIDE))
-    eye = lax.broadcasted_iota(jnp.int32, (SIDE, SIDE), 0) == lax.broadcasted_iota(jnp.int32, (SIDE, SIDE), 1)
-    return jnp.broadcast_to(jnp.sum(jnp.where(eye, row, 0.0), axis=1, keepdims=True), (SIDE, LANES))
-
-
 def up(v, count, axis):
     return pltpu.roll(v, v.shape[axis] - count, axis)
 
@@ -311,11 +305,6 @@
     return [[cols[j][i] for j in range(4)] for i in range(4)]
 
 
-def element_rows(mix, er, i, which):
-    start = er * 64 + which * 16 + i * 4
-    return mix.at[pl.ds(start, 4)], mix.at[pl.ds(start + 32, 4)]
-
-
 def spread(mix, plane, er, i, which, v):
     for ec in range(2):
         mix[plane, pl.ds(er * 64 + ec * 32 + which * 16 + i * 4, 4), :] = v[4 * ec : 4 * ec + 4]
@@ -328,6 +317,14 @@
 def main_kernel(
     groups,
     blocks,
+    nbr_face_in,
+    nbr_edge_in,
+    state_in,
+    jac_in,
+    diag_in,
+    cross_in,
+    coriolis_in,
+    out,
     nbr_face,
     nbr_edge,
     state,
@@ -335,7 +332,6 @@
     diag,
     cross,
     coriolis,
-    out,
     mix,
     send,
     send_geo,
@@ -344,6 +340,7 @@
     coef,
     section,
     back,
+    sem_load,
     sem_s_geo,
     sem_r_geo,
     sem_s_in,
@@ -360,17 +357,39 @@
     x = lax.axis_index("fx")
     me = (g * blocks + y) * blocks + x
 
-    def others():
-        for dx in (2, 3, 1, 0):
-            for dy in range(blocks):
-                for dg in range(groups):
-                    if dx or dy or dg:
-                        at = (lax.rem(g + dg, groups), lax.rem(y + dy, blocks), lax.rem(x + dx, blocks))
-                        yield (at[0] * blocks + at[1]) * blocks + at[2], at
-
+    def by_distance(at):
+        return [last - at, lax.rem(at + 2, 4), at + 1 - 2 * lax.rem(at, 2), at]
+
+    def others(ys=(0, 1, 2, 3)):
+        for k, tx in enumerate(by_distance(x)):
+            for n in ys:
+                ty = by_distance(y)[n]
+                for dg in (1, 0):
+                    if k < 3 or n < 3 or dg:
+                        tg = lax.rem(g + dg, groups)
+                        yield (tg * blocks + ty) * blocks + tx, (tg, ty, tx)
+
+    loads = [
+        pltpu.make_async_copy(src, dst, sem_load.at[n])
+        for n, (src, dst) in enumerate(
+            (
+                (state_in, state),
+                (jac_in, jac),
+                (diag_in, diag),
+                (cross_in, cross),
+                (coriolis_in, coriolis),
+                (nbr_face_in, nbr_face),
+                (nbr_edge_in, nbr_edge),
+            )
+        )
+    ]
     barrier = pltpu.get_barrier_semaphore()
     for _, at in others():
         pl.semaphore_signal(barrier, inc=1, device_id=at, device_id_type=MESH)
+    for load in loads:
+        load.start()
+    for load in loads[1:]:
+        load.wait()
 
     sub = lax.broadcasted_iota(jnp.int32, (SIDE, LANES), 0)
     lane = lax.broadcasted_iota(jnp.int32, (SIDE, LANES), 1)
@@ -380,15 +399,14 @@
     weights = (1.0 / 6.0, 5.0 / 6.0, 5.0 / 6.0, 1.0 / 6.0)
     zero = jnp.zeros((SIDE, LANES), jnp.float32)
 
-    def per_node(entries):
-        total = jnp.full((SIDE, LANES), entries[0], jnp.float32)
-        for j in range(1, 4):
-            total = jnp.where(node == j, jnp.float32(entries[j]), total)
+    def per_node(entries, at):
+        total = jnp.full(at.shape, entries[0], jnp.float32)
+        for n in range(1, 4):
+            total = jnp.where(at == n, jnp.float32(entries[n]), total)
         return total
 
-    col_weight = per_node(weights)
     taps = {
-        s: per_node([float(table[j, j + s]) if 0 <= j + s < 4 else 0.0 for j in range(4)])
+        s: per_node([float(table[n, n + s]) if 0 <= n + s < 4 else 0.0 for n in range(4)], node)
         for s in range(-3, 4)
     }
 
@@ -401,56 +419,77 @@
             total = total + taps[s] * pltpu.roll(v, (-s) % SIDE, 0)
         return total
 
-    second = (lane >= 32) & (lane < 64)
-    geo = [[[None, None] for _ in range(SIDE)] for _ in range(faces)]
+    def pick(v, at):
+        return jnp.take_along_axis(v, at, axis=1, mode="promise_in_bounds")
+
+    def spread_lanes(tiles):
+        tiles = tiles + [tiles[0]] * (LANES // SIDE - len(tiles))
+        return jnp.concatenate(tiles, axis=0).T
+
+    tile_sub = lax.broadcasted_iota(jnp.int32, (SIDE, SIDE), 0) % 4
+    tile_lane = lax.broadcasted_iota(jnp.int32, (SIDE, SIDE), 1) % 4
+    tile_weight = per_node(weights, tile_sub) * per_node(weights, tile_lane)
+    near_tiles, far_tiles = [], []
     for f in range(faces):
-        for start in range(0, SIDE, 4):
-            wind, temp, contra, energy, vol, cor, mass = [], [], [], [], [], [], []
-            for r in range(start, start + 4):
-                j = widen(jac, (f,), r)
-                m_xx, m_yy, m_xy = widen(diag, (0, f), r), widen(diag, (1, f), r), widen(cross, (f,), r)
-                w = state[f, r, :, 0 : 2 * HALF]
-                t = state[f, r, :, 2 * HALF : 3 * HALF]
-                t = jnp.concatenate([t, t], axis=1)
-                c = jnp.where(low, m_xx, m_yy) * w + m_xy * swap(w)
-                p = w * c
-                wind.append(w)
-                temp.append(t)
-                contra.append(c)
-                energy.append(0.5 * (p + swap(p)) + t)
-                vol.append(j)
-                cor.append(widen(coriolis, (f,), r))
-                mass.append(j * (jnp.float32(weights[r % 4]) * col_weight))
-                even = lane % 2 == 0
-                geo[f][r][0] = jnp.where(even, j * m_xx, j * m_yy)
-                geo[f][r][1] = jnp.where(even, j * m_xy, mass[-1])
-            dxs = [along_sub(jnp.where(low, energy[i], wind[i])) for i in range(4)]
-            dys = slope([jnp.where(low, wind[i], energy[i]) for i in range(4)])
-            dxt = [along_sub(temp[i]) for i in range(4)]
-            dyt = slope(temp)
-            for i in range(4):
-                dxv = jnp.where(low, swap(dxs[i]), dxs[i])
-                dyu = jnp.where(low, dys[i], swap(dys[i]))
-                spin = (dxv - dyu) + cor[i] * vol[i]
-                spin = jnp.where(low, spin, -spin)
-                tend = spin * swap(contra[i]) - jnp.where(low, dxs[i], dys[i])
-                fresh = mass[i] * (wind[i] + time_step * tend)
-                q = contra[i] * jnp.where(low, dxt[i], dyt[i])
-                heat = mass[i] * (temp[i] - time_step * (q + swap(q)))
-                er = start // 4
-                spread(mix, f, er, i, 0, jnp.where(second, down(heat, 32, 1), fresh))
-                spread(mix, f, er, i, 1, jnp.where(second, heat, up(fresh, 32, 1)))
+        vol, m_xx, m_yy, m_xy = jac[f], diag[0, f], diag[1, f], cross[f]
+        mass = vol * tile_weight
+        near_tiles += [m_xx, m_yy, m_xy, vol * coriolis[f], mass]
+        far_tiles += [vol * m_xx, vol * m_yy, vol * m_xy, mass]
+    local, shared = spread_lanes(near_tiles), spread_lanes(far_tiles)
+
+    def spot(f, k, r):
+        return (f * 5 + k) * SIDE + r
+
+    cells = [(f, r) for f in range(faces) for r in range(SIDE)]
+    lines = [[n + i for i in range(4)] for n in range(0, len(cells), 4)]
     for r in range(SIDE):
         for h in range(2):
-            v = geo[0][r][h]
-            for f in range(1, faces):
-                v = jnp.where(lane >= 2 * f, geo[f][r][h], v)
-            spread(mix, faces, r // 4, r % 4, h, v)
+            at = (lane // 2 % faces) * (4 * SIDE) + (2 * h + lane % 2) * SIDE + r
+            spread(mix, faces, r // 4, r % 4, h, pick(shared, at))
+    own = [pick(local, jnp.where(low, spot(f, 0, r), spot(f, 1, r))) for f, r in cells]
+    skew = [pick(local, lane * 0 + spot(f, 2, r)) for f, r in cells]
+    turn = [pick(local, lane * 0 + spot(f, 3, r)) for f, r in cells]
+    mass = [pick(local, lane * 0 + spot(f, 4, r)) for f, r in cells]
+    send_geo[...] = by_node(mix, faces).T[0:SIDE]
+    loads[0].wait()
+    wind = [state[f, r, :, 0 : 2 * HALF] for f, r in cells]
+    temp = [state[f, r, :, 2 * HALF : 3 * HALF] for f, r in cells]
+    temp = [jnp.concatenate([t, t], axis=1) for t in temp]
+    other = [swap(w) for w in wind]
+    contra = [m * w + n * o for m, n, w, o in zip(own, skew, wind, other)]
+    power = [w * c for w, c in zip(wind, contra)]
+    crossed = [swap(c) for c in contra]
+    turned = [swap(p) for p in power]
+    energy = [0.5 * (p + q) + t for p, q, t in zip(power, turned, temp)]
+
+    def down_lines(v):
+        out = [None] * len(cells)
+        for line in lines:
+            for n, d in zip(line, slope([v[n] for n in line])):
+                out[n] = d
+        return out
+
+    dxs = [along_sub(jnp.where(low, e, w)) for e, w in zip(energy, wind)]
+    dys = down_lines([jnp.where(low, w, e) for e, w in zip(energy, wind)])
+    flow = [c * jnp.where(low, a, b) for c, a, b in zip(contra, [along_sub(t) for t in temp], down_lines(temp))]
+    dxv = [swap(a) for a in dxs]
+    dyu = [swap(a) for a in dys]
+    flow = [q + swap(q) for q in flow]
+    heat = [m * (t - time_step * q) for m, t, q in zip(mass, temp, flow)]
+    fresh = []
+    for n in range(len(cells)):
+        spin = jnp.where(low, dxv[n] - dys[n], dyu[n] - dxs[n]) + jnp.where(low, turn[n], -turn[n])
+        tend = spin * crossed[n] - jnp.where(low, dxs[n], dys[n])
+        fresh.append(mass[n] * (wind[n] + time_step * tend))
+    second = (lane >= 32) & (lane < 64)
+    shifted = [(down(t, 32, 1), up(w, 32, 1)) for t, w in zip(heat, fresh)]
+    for n, (f, r) in enumerate(cells):
+        spread(mix, f, r // 4, r % 4, 0, jnp.where(second, shifted[n][0], fresh[n]))
+        spread(mix, f, r // 4, r % 4, 1, jnp.where(second, heat[n], shifted[n][1]))
     for f in range(faces):
         turned = by_node(mix, f).T
         for k, part in enumerate((0, 2, 1)):
             send[k * faces + f] = turned[part * count : (part + 1) * count]
-    send_geo[...] = by_node(mix, faces).T[0:SIDE]
 
     er, ec, lev = sub // 4, (sub // 2) % 2, sub % 2
     lx, ly = lane % blocks, (lane // blocks) % blocks
@@ -500,16 +539,6 @@
     def prev_col(v):
         return jnp.where(ec1, down(v, 2, 0), jnp.where(x_lo, zero, down(up(v, 2, 0), 1, 1)))
 
-    def within(v):
-        v = [list(row) for row in v]
-        for j in range(4):
-            a, b = v[0][j], v[3][j]
-            v[0][j], v[3][j] = a + prev_row(b), b + next_row(a)
-        for i in range(4):
-            a, b = v[i][0], v[i][3]
-            v[i][0], v[i][3] = a + prev_col(b), b + next_col(a)
-        return v
-
     def rims(v):
         found = []
         for b in range(4):
@@ -518,9 +547,7 @@
             tall = jnp.where(x_hi, v[b][3], v[b][0])
             tall = jnp.where(ec0 == x_hi, jnp.where(x_hi, up(tall, 2, 0), down(tall, 2, 0)), tall)
             tall = jnp.where(er == ec, tall, down(tall, 4, 0))
-            flat = jnp.take_along_axis(flat, source_at, axis=1, mode="promise_in_bounds")
-            tall = jnp.take_along_axis(tall, source_at, axis=1, mode="promise_in_bounds")
-            found.append(jnp.where(from_flat, flat, tall))
+            found.append(jnp.where(from_flat, pick(flat, source_at), pick(tall, source_at)))
         partner = []
         for b in range(4):
             w = found[3 - b]
@@ -528,28 +555,33 @@
             partner.append(jnp.where(flipped, w, found[b]))
         return partner
 
-    def add_rims(v, partner):
-        for b in range(4):
-            p = partner[b]
+    def glue(v, partner):
+        v = [list(row) for row in v]
+        sides = []
+        for j in range(4):
+            a, b, p = v[0][j], v[3][j], partner[j]
             s = down(p, 4, 0)
-            v[0][b] = v[0][b] + jnp.where(edge_at[0], p, zero)
-            v[3][b] = v[3][b] + jnp.where(er1 & y_hi, s, zero)
+            v[0][j] = a + jnp.where(edge_at[0], p, prev_row(b))
+            v[3][j] = b + jnp.where(er1 & y_hi, s, next_row(a))
             q = jnp.where(er1, p, s)
             q = jnp.where(er == ec, q, jnp.where(er0, down(q, 2, 0), up(q, 2, 0)))
-            v[b][0] = v[b][0] + jnp.where(ec0 & x_lo, q, zero)
-            v[b][3] = v[b][3] + jnp.where(ec1 & x_hi, q, zero)
+            sides.append(q)
+        q0, q3 = sides[0], sides[3]
+        sides[0], sides[3] = q0 + prev_row(q3), q3 + next_row(q0)
+        for i in range(4):
+            a, b, q = v[i][0], v[i][3], sides[i]
+            v[i][0] = a + jnp.where(ec0 & x_lo, q, prev_col(b))
+            v[i][3] = b + jnp.where(ec1 & x_hi, q, next_col(a))
         return v
 
     def assemble_one(v):
-        v = within(v)
-        return add_rims(v, rims(v))
+        return glue(v, rims(v))
 
     def assemble_pair(u, v):
-        u, v = within(u), within(v)
         pu, pv = rims(u), rims(v)
         tu = [cosine * a - sine * b for a, b in zip(pu, pv)]
         tv = [sine * a + cosine * b for a, b in zip(pu, pv)]
-        return add_rims(u, tu), add_rims(v, tv)
+        return glue(u, tu), glue(v, tv)
 
     def grid(flat):
         return [[flat[8 * (4 * i + j) : 8 * (4 * i + j) + 8] for j in range(4)] for i in range(4)]
@@ -570,8 +602,8 @@
     def each(fn, *vs):
         return [[fn(*(v[i][j] for v in vs)) for j in range(4)] for i in range(4)]
 
-    def copies(src_of, dst, sem_s, sem_r):
-        for d, at in others():
+    def copies(src_of, dst, sem_s, sem_r, ys=(0, 1, 2, 3)):
+        for d, at in others(ys):
             pltpu.make_async_remote_copy(
                 src_ref=src_of(d),
                 dst_ref=dst,
@@ -581,8 +613,9 @@
                 device_id_type=MESH,
             ).start()
 
-    def all_of(ref, sem_s, sem_r):
-        part = ref.at[:, pl.ds(0, count - 1)]
+    def all_of(ref, sem_s, sem_r, first=0, planes=None, rows=None):
+        planes = ref.shape[0] if planes is None else planes
+        part = ref.at[pl.ds(first, planes), pl.ds(0, rows or count - 1)]
         return pltpu.make_async_remote_copy(
             src_ref=part,
             dst_ref=part,
@@ -593,15 +626,60 @@
         )
 
     pairs = 2 * faces
+    half = count // 2
+    parts = ((2 * faces, faces), (0, 2 * faces))
     pl.semaphore_wait(barrier, count - 1)
-    copies(lambda d: send_geo.at[pl.ds(0, pairs)], got_geo.at[:, me], sem_s_geo, sem_r_geo)
-    copies(lambda d: send.at[:, d], got.at[:, me], sem_s_in, sem_r_in)
-    for q in range(pairs):
-        got_geo[q, pl.ds(me, 1), :] = send_geo[pl.ds(q, 1), :]
+    odd = lax.rem(y, 2) == 1
+    even = jnp.logical_not(odd)
+
+    def send_shape(at):
+        pltpu.make_async_remote_copy(
+            src_ref=send_geo.at[pl.ds(0, pairs)],
+            dst_ref=got_geo.at[:, me],
+            send_sem=sem_s_geo.at[0],
+            recv_sem=sem_r_geo.at[0],
+            device_id=at,
+            device_id_type=MESH,
+        ).start()
+
+    for k, tx in enumerate(by_distance(x)):
+        for ty in (3 - y // 2 * 2, y // 2 * 2 + 1):
+            for tg in (lax.rem(g + 1, groups), g):
+                send_to = functools.partial(send_shape, (tg, ty, tx))
+                if k == 3 and tg is g:
+                    pl.when(jnp.logical_not((ty == y) & odd))(send_to)
+                else:
+                    send_to()
+    for n, (first, planes) in enumerate(parts):
+        part = pl.ds(first, planes)
+        copies(lambda d: send.at[part, d], got.at[part, me], sem_s_in.at[n], sem_r_in.at[n])
+
+    @pl.when(odd)
+    def _():
+        for q in range(pairs):
+            got_geo[q, pl.ds(me, 1), :] = send_geo[pl.ds(q, 1), :]
+
     for q in range(3 * faces):
         got[q, pl.ds(me, 1), :] = send[q, pl.ds(me, 1), :]
 
-    all_of(got_geo, sem_s_geo, sem_r_geo).wait_recv()
+    relay = pltpu.make_async_remote_copy(
+        src_ref=got_geo,
+        dst_ref=got_geo,
+        send_sem=sem_s_geo.at[1],
+        recv_sem=sem_r_geo.at[1],
+        device_id=(g, y + 1 - 2 * lax.rem(y, 2), x),
+        device_id_type=MESH,
+    )
+
+    def shapes(rows):
+        return all_of(got_geo, sem_s_geo.at[0], sem_r_geo.at[0], rows=rows)
+
+    @pl.when(odd)
+    def _():
+        shapes(count - 1).wait_recv()
+        relay.start()
+
+    pl.when(even)(relay.wait_recv)
     for p in range(2):
         both = receive(got_geo, range(p, pairs, 2))
         put(coef, 2 * p, each(lambda v: jnp.where(lev == 0, v, down(v, 1, 0)), both))
@@ -635,23 +713,35 @@
         own.start()
         return own
 
-    all_of(got, sem_s_in, sem_r_in).wait_recv()
+    def arrived(n):
+        first, planes = parts[n]
+        return all_of(got, sem_s_in.at[n], sem_r_in.at[n], first, planes)
+
+    arrived(0).wait_recv()
     heat = scaled(assemble_one(fields_in(2)))
     put(section, 2, heat)
-    wind_u, wind_v = assemble_pair(fields_in(0), fields_in(1))
-    put(section, 0, scaled(wind_u))
-    put(section, 1, scaled(wind_v))
     heat = scaled(assemble_one(laplace_of(heat)))
     heat = scaled(assemble_one(laplace_of(heat)))
     finish(2, heat)
     own_t = send_back(2, 1)
+    arrived(1).wait_recv()
+    wind_u, wind_v = assemble_pair(fields_in(0), fields_in(1))
+    put(section, 0, scaled(wind_u))
+    put(section, 1, scaled(wind_v))
     wind_u, wind_v = assemble_pair(laplace_of(take(section, 0)), laplace_of(take(section, 1)))
     wind_u, wind_v = assemble_pair(laplace_of(scaled(wind_u)), laplace_of(scaled(wind_v)))
     finish(0, scaled(wind_u))
     finish(1, scaled(wind_v))
     own_w = send_back(0, 2)
-    all_of(got_geo, sem_s_geo, sem_r_geo).wait_send()
-    all_of(got, sem_s_in, sem_r_in).wait_send()
+
+    @pl.when(odd)
+    def _():
+        shapes(half - 1).wait_send()
+        relay.wait_send()
+
+    pl.when(even)(shapes(half).wait_send)
+    arrived(0).wait_send()
+    arrived(1).wait_send()
     own_t.wait()
     own_w.wait()
     all_of(out, sem_s_out, sem_r_out).wait_send()
@@ -680,16 +770,20 @@
 def by_level(groups, blocks, state, jacobian, metric_diag, metric_cross, coriolis, nbr_face, nbr_edge):
     faces = state.shape[0]
     count = groups * blocks * blocks
-    vmem, smem = pl.BlockSpec(memory_space=pltpu.VMEM), pl.BlockSpec(memory_space=pltpu.SMEM)
+    vmem, anywhere = pl.BlockSpec(memory_space=pltpu.VMEM), pl.BlockSpec(memory_space=pl.ANY)
+    inputs = (nbr_face.T, nbr_edge.T, state, jacobian, metric_diag, metric_cross, coriolis)
+    inputs = [pltpu.with_memory_space_constraint(a, pltpu.HBM) for a in inputs]
     piece = (3 * faces, count, LANES)
     cells = (4, 4, SIDE, LANES)
     dma = pltpu.SemaphoreType.DMA
     got = pl.pallas_call(
         functools.partial(main_kernel, groups, blocks),
         out_shape=jax.ShapeDtypeStruct(piece, jnp.float32),
-        in_specs=[smem, smem] + [vmem] * 5,
-        out_specs=pl.BlockSpec(memory_space=pltpu.HBM),
-        scratch_shapes=[
+        in_specs=[pl.BlockSpec(memory_space=pltpu.HBM)] * 7,
+        out_specs=anywhere,
+        scratch_shapes=[pltpu.SMEM(a.shape, a.dtype) for a in inputs[:2]]
+        + [pltpu.VMEM(a.shape, a.dtype) for a in inputs[2:]]
+        + [
             pltpu.VMEM((faces + 1, LANES, LANES), jnp.float32),
             pltpu.VMEM(piece, jnp.float32),
             pltpu.VMEM((SIDE, LANES), jnp.float32),
@@ -699,16 +793,16 @@
             pltpu.VMEM((3,) + cells, jnp.float32),
             pltpu.VMEM(piece, jnp.float32),
         ]
-        + [dma] * 6
-        + [dma((3,))],
-        compiler_params=pltpu.CompilerParams(collective_id=0, has_side_effects=True),
-    )(nbr_face.T, nbr_edge.T, state, jacobian, metric_diag, metric_cross, coriolis)
+        + [dma((7,)), dma((2,)), dma((2,)), dma((2,)), dma((2,)), dma, dma, dma((3,))],
+        compiler_params=pltpu.CompilerParams(collective_id=0, has_side_effects=True, vmem_limit_bytes=16 << 20),
+    )(*inputs)
     return pl.pallas_call(
         last_kernel,
         out_shape=jax.ShapeDtypeStruct(state.shape, jnp.float32),
         in_specs=[vmem],
         out_specs=vmem,
         scratch_shapes=[pltpu.VMEM((faces, LANES, LANES), jnp.float32)],
+        compiler_params=pltpu.CompilerParams(vmem_limit_bytes=16 << 20),
     )(got)
 
 

time: 25.4 us -> 20.5 us (0.81)
  Pallas kernels: 25.2 us -> 20.3 us
    pallas_call x1, Pallas kernels: 23.3 us -> 19.4 us  [by_level(): pl.pallas_call(functools.partial(main_kernel, groups, blocks), out_shape=...]
    pallas_call x1, Pallas kernels: 1.83 us -> 0.92 us  [by_level(): pl.pallas_call(last_kernel, out_shape=jax.ShapeDtypeStruct(state.shape, j...]
where the time goes in v1:
time: 20.5 us; the launch traced here: 20.3 us
  Pallas kernels  20.3 us (99%)
    pallas_call x1, Pallas kernels, by_level(): pl.pallas_call(functools.partial(main_kernel, groups, blocks), out_shape=...  19.4 us
    pallas_call x1, Pallas kernels, by_level(): pl.pallas_call(last_kernel, out_shape=jax.ShapeDtypeStruct(state.shape, j...  0.92 us

profile of v1, /device:TPU:0, one launch (start us, length us, event | category | flops | bytes accessed | tf_op | source)
XLA Modules:
  0.0 20.3 jit_solution(12304840610142813026)
XLA Ops:
  0.0 19.4 %shard_map.73.got = f32[9,32,128]{2,1,0:T(8,128)S(1)} custom-call(s32[4,6]{1,0:T(4,128)} %bitcast.2, s32[4,6]{1,0:T(4,128)} %bitcast.3, f32[3,8,8,192]{3,2,1,0:T(8,128)} %state_in.1, f32[3,8,8]{2,1,0:T(8,128)} %jac_in.1, f32[2,3,8,8]{3,2,1,0:T(8,128)} %diag_in.1, f32[3,8,8]{2,1,0:T(8,128)} %cross_in.1, f32[3,8,8]{2,1,0:T(8,128)} %coriolis_in.1), custom_call_target="tpu_custom_call" | custom-call | tf_op jit(solution)/shard_map/pallas_call | solution.py:779
  19.4 0.9 %shard_map.74 = f32[3,8,8,192]{3,2,1,0:T(8,128)} custom-call(f32[9,32,128]{2,1,0:T(8,128)S(1)} %shard_map.73.got), custom_call_target="tpu_custom_call" | custom-call | tf_op jit(solution)/shard_map/pallas_call | solution.py:799

commit v2 on v1

--- a/solution.py
+++ b/solution.py
@@ -275,6 +275,10 @@
 SIDE = 8
 HALF = 64
 LANES = 128
+
+
+IN_KINDS = "gggtttwwwgtw"
+IN_COLUMNS = ("321321321000", "320320320111", "301301301222", "012012012333")
 
 
 def up(v, count, axis):
@@ -360,14 +364,18 @@
     def by_distance(at):
         return [last - at, lax.rem(at + 2, 4), at + 1 - 2 * lax.rem(at, 2), at]
 
-    def others(ys=(0, 1, 2, 3)):
-        for k, tx in enumerate(by_distance(x)):
-            for n in ys:
-                ty = by_distance(y)[n]
-                for dg in (1, 0):
-                    if k < 3 or n < 3 or dg:
-                        tg = lax.rem(g + dg, groups)
+    def others(columns):
+        for n, tx in enumerate(columns):
+            for ty in by_distance(y)[: blocks - 1] + [y]:
+                for tg in (lax.rem(g + 1, groups), g):
+                    if tx is not x or ty is not y or tg is not g:
                         yield (tg * blocks + ty) * blocks + tx, (tg, ty, tx)
+
+    def towards(columns):
+        for tx in columns:
+            for ty in range(blocks):
+                for tg in range(groups):
+                    yield (tg * blocks + ty) * blocks + tx, (tg, ty, tx)
 
     loads = [
         pltpu.make_async_copy(src, dst, sem_load.at[n])
@@ -384,7 +392,7 @@
         )
     ]
     barrier = pltpu.get_barrier_semaphore()
-    for _, at in others():
+    for _, at in others(by_distance(x)):
         pl.semaphore_signal(barrier, inc=1, device_id=at, device_id_type=MESH)
     for load in loads:
         load.start()
@@ -602,16 +610,15 @@
     def each(fn, *vs):
         return [[fn(*(v[i][j] for v in vs)) for j in range(4)] for i in range(4)]
 
-    def copies(src_of, dst, sem_s, sem_r, ys=(0, 1, 2, 3)):
-        for d, at in others(ys):
-            pltpu.make_async_remote_copy(
-                src_ref=src_of(d),
-                dst_ref=dst,
-                send_sem=sem_s,
-                recv_sem=sem_r,
-                device_id=at,
-                device_id_type=MESH,
-            ).start()
+    def copy_to(at, src, dst, sem_s, sem_r):
+        pltpu.make_async_remote_copy(
+            src_ref=src,
+            dst_ref=dst,
+            send_sem=sem_s,
+            recv_sem=sem_r,
+            device_id=at,
+            device_id_type=MESH,
+        ).start()
 
     def all_of(ref, sem_s, sem_r, first=0, planes=None, rows=None):
         planes = ref.shape[0] if planes is None else planes
@@ -632,35 +639,36 @@
     odd = lax.rem(y, 2) == 1
     even = jnp.logical_not(odd)
 
-    def send_shape(at):
-        pltpu.make_async_remote_copy(
-            src_ref=send_geo.at[pl.ds(0, pairs)],
-            dst_ref=got_geo.at[:, me],
-            send_sem=sem_s_geo.at[0],
-            recv_sem=sem_r_geo.at[0],
-            device_id=at,
-            device_id_type=MESH,
-        ).start()
-
-    for k, tx in enumerate(by_distance(x)):
-        for ty in (3 - y // 2 * 2, y // 2 * 2 + 1):
-            for tg in (lax.rem(g + 1, groups), g):
-                send_to = functools.partial(send_shape, (tg, ty, tx))
-                if k == 3 and tg is g:
-                    pl.when(jnp.logical_not((ty == y) & odd))(send_to)
-                else:
-                    send_to()
-    for n, (first, planes) in enumerate(parts):
-        part = pl.ds(first, planes)
-        copies(lambda d: send.at[part, d], got.at[part, me], sem_s_in.at[n], sem_r_in.at[n])
+    def send_shapes(c):
+        for d, at in towards([c]):
+            if at[1] % 2 == 1:
+                src, dst = send_geo.at[pl.ds(0, pairs)], got_geo.at[:, me]
+                pl.when(d != me)(functools.partial(copy_to, at, src, dst, sem_s_geo.at[0], sem_r_geo.at[0]))
+
+    def send_part(n, c):
+        part = pl.ds(*parts[n])
+        for d, at in towards([c]):
+            src, dst = send.at[part, d], got.at[part, me]
+            pl.when(d != me)(functools.partial(copy_to, at, src, dst, sem_s_in.at[n], sem_r_in.at[n]))
+
+    def send_from(column):
+        for kind, c in zip(IN_KINDS, map(int, IN_COLUMNS[column])):
+            if kind == "g":
+                send_shapes(c)
+            else:
+                send_part("tw".index(kind), c)
+
+    for column in range(blocks):
+        pl.when(x == column)(functools.partial(send_from, column))
+
+    for q in range(3 * faces):
+        got[q, pl.ds(me, 1), :] = send[q, pl.ds(me, 1), :]
 
     @pl.when(odd)
     def _():
         for q in range(pairs):
             got_geo[q, pl.ds(me, 1), :] = send_geo[pl.ds(q, 1), :]
 
-    for q in range(3 * faces):
-        got[q, pl.ds(me, 1), :] = send[q, pl.ds(me, 1), :]
 
     relay = pltpu.make_async_remote_copy(
         src_ref=got_geo,
@@ -706,12 +714,16 @@
         for f in range(faces):
             back[k * faces + f] = turned[f * count : (f + 1) * count]
 
-    def send_back(k, n):
-        part = pl.ds(k * faces, n * faces)
-        copies(lambda d: back.at[part, d], out.at[part, me], sem_s_out, sem_r_out)
-        own = pltpu.make_async_copy(back.at[part, me], out.at[part, me], sem_own.at[k])
-        own.start()
-        return own
+    def send_back(n):
+        part = pl.ds(*parts[n])
+        for d, at in towards(range(blocks)):
+            pl.when(d != me)(
+                functools.partial(copy_to, at, back.at[part, d], out.at[part, me], sem_s_out, sem_r_out)
+            )
+
+    def kept(n):
+        part = pl.ds(*parts[n])
+        return pltpu.make_async_copy(back.at[part, me], out.at[part, me], sem_own.at[n])
 
     def arrived(n):
         first, planes = parts[n]
@@ -723,7 +735,8 @@
     heat = scaled(assemble_one(laplace_of(heat)))
     heat = scaled(assemble_one(laplace_of(heat)))
     finish(2, heat)
-    own_t = send_back(2, 1)
+    send_back(0)
+    kept(0).start()
     arrived(1).wait_recv()
     wind_u, wind_v = assemble_pair(fields_in(0), fields_in(1))
     put(section, 0, scaled(wind_u))
@@ -732,7 +745,8 @@
     wind_u, wind_v = assemble_pair(laplace_of(scaled(wind_u)), laplace_of(scaled(wind_v)))
     finish(0, scaled(wind_u))
     finish(1, scaled(wind_v))
-    own_w = send_back(0, 2)
+    send_back(1)
+    kept(1).start()
 
     @pl.when(odd)
     def _():
@@ -742,29 +756,36 @@
     pl.when(even)(shapes(half).wait_send)
     arrived(0).wait_send()
     arrived(1).wait_send()
-    own_t.wait()
-    own_w.wait()
+    kept(0).wait()
+    kept(1).wait()
     all_of(out, sem_s_out, sem_r_out).wait_send()
     all_of(out, sem_s_out, sem_r_out).wait_recv()
 
 
-def last_kernel(got, out, mix):
-    faces = out.shape[0]
+def last_kernel(got, out, mix, full, sem):
+    faces = full.shape[0]
     lane = lax.broadcasted_iota(jnp.int32, (SIDE, LANES), 1)
-    even = (lane // 32) % 2 == 0
+    first = (lane // 32) % 2 == 0
+
+    def half_rows(n, f, r, h):
+        start = (r % 4) * 32 + (r // 4) * 4 + h
+        return jnp.concatenate([mix[n, f, pl.ds(start + ec * 2, 4, stride=8), :] for ec in range(2)], axis=0)
+
+    def copy_of(f):
+        return pltpu.make_async_copy(full.at[f], out.at[f], sem.at[f])
+
     for f in range(faces):
         u, v, t = (got[k * faces + f] for k in range(3))
-        turned = jnp.concatenate([u, t, v, v], axis=0).T
-        for n in range(16):
-            mix[f, pl.ds(n, 8, stride=16), :] = turned[8 * n : 8 * n + 8]
+        for m, parts in enumerate(((u, u, v, v), (t, t, t, t))):
+            mix[m, f] = jnp.concatenate(parts, axis=0).T
+    for f in range(faces):
         for r in range(SIDE):
-            start = (r // 4) * 64 + (r % 4) * 4
-            a, b = (
-                jnp.concatenate([mix[f, pl.ds(start + h * 16 + ec * 32, 4), :] for ec in range(2)], axis=0)
-                for h in range(2)
-            )
-            out[f, r, :, 0 : 2 * HALF] = jnp.where(even, a, down(b, 32, 1))
-            out[f, r, :, 2 * HALF : 3 * HALF] = jnp.where(even, up(a, 32, 1), b)[:, 0:HALF]
+            wind, temp = (jnp.where(first, half_rows(m, f, r, 0), half_rows(m, f, r, 1)) for m in range(2))
+            full[f, r, :, 0 : 2 * HALF] = wind
+            full[f, r, :, 2 * HALF : 3 * HALF] = temp[:, 0:HALF]
+        copy_of(f).start()
+    for f in range(faces):
+        copy_of(f).wait()
 
 
 def by_level(groups, blocks, state, jacobian, metric_diag, metric_cross, coriolis, nbr_face, nbr_edge):
@@ -800,8 +821,12 @@
         last_kernel,
         out_shape=jax.ShapeDtypeStruct(state.shape, jnp.float32),
         in_specs=[vmem],
-        out_specs=vmem,
-        scratch_shapes=[pltpu.VMEM((faces, LANES, LANES), jnp.float32)],
+        out_specs=anywhere,
+        scratch_shapes=[
+            pltpu.VMEM((2, faces, LANES, LANES), jnp.float32),
+            pltpu.VMEM(state.shape, jnp.float32),
+            dma((faces,)),
+        ],
         compiler_params=pltpu.CompilerParams(vmem_limit_bytes=16 << 20),
     )(got)
 

time: 20.5 us -> 20.1 us (0.980)
  Pallas kernels: 20.3 us -> 20 us
    pallas_call x1, Pallas kernels: 19.4 us -> 19.1 us  [by_level(): pl.pallas_call(functools.partial(main_kernel, groups, blocks), out_shape=...]
where the time goes in v2:
time: 20.1 us; the launch traced here: 20 us
  Pallas kernels  20 us (100%)
    pallas_call x1, Pallas kernels, by_level(): pl.pallas_call(functools.partial(main_kernel, groups, blocks), out_shape=...  19.1 us
    pallas_call x1, Pallas kernels, by_level(): pl.pallas_call(last_kernel, out_shape=jax.ShapeDtypeStruct(state.shape, j...  0.86 us

profile of v2, /device:TPU:0, one launch (start us, length us, event | category | flops | bytes accessed | tf_op | source)
XLA Modules:
  0.0 20.0 jit_solution(17662542689840394641)
XLA Ops:
  0.0 19.1 %shard_map.73.got = f32[9,32,128]{2,1,0:T(8,128)S(1)} custom-call(s32[4,6]{1,0:T(4,128)} %bitcast.2, s32[4,6]{1,0:T(4,128)} %bitcast.3, f32[3,8,8,192]{3,2,1,0:T(8,128)} %state_in.1, f32[3,8,8]{2,1,0:T(8,128)} %jac_in.1, f32[2,3,8,8]{3,2,1,0:T(8,128)} %diag_in.1, f32[3,8,8]{2,1,0:T(8,128)} %cross_in.1, f32[3,8,8]{2,1,0:T(8,128)} %coriolis_in.1), custom_call_target="tpu_custom_call" | custom-call | tf_op jit(solution)/shard_map/pallas_call | solution.py:800
  19.1 0.9 %shard_map.74 = f32[3,8,8,192]{3,2,1,0:T(8,128)} custom-call(f32[9,32,128]{2,1,0:T(8,128)S(1)} %shard_map.73.got), custom_call_target="tpu_custom_call" | custom-call | tf_op jit(solution)/shard_map/pallas_call | solution.py:820

commit v3 on v2

--- a/solution.py
+++ b/solution.py
@@ -289,23 +289,28 @@
     return pltpu.roll(v, count, axis)
 
 
-def slope(a):
+def slope_size():
     d = deriv_table()
+    return (d[0, 0] + d[0, 3]) / 2
+
+
+def slope(a, size=1.0):
+    d = deriv_table() / (2 * size)
     p0, p1, m0, m1 = a[0] + a[3], a[1] + a[2], a[0] - a[3], a[1] - a[2]
     bend = p0 - p1
-    o0 = jnp.float32((d[0, 0] + d[0, 3]) / 2) * bend
-    o1 = jnp.float32((d[1, 0] + d[1, 3]) / 2) * bend
-    q0 = jnp.float32((d[0, 0] - d[0, 3]) / 2) * m0 + jnp.float32((d[0, 1] - d[0, 2]) / 2) * m1
-    q1 = jnp.float32((d[1, 0] - d[1, 3]) / 2) * m0 + jnp.float32((d[1, 1] - d[1, 2]) / 2) * m1
+    o0 = bend if size != 1.0 else jnp.float32(d[0, 0] + d[0, 3]) * bend
+    o1 = jnp.float32(d[1, 0] + d[1, 3]) * bend
+    q0 = jnp.float32(d[0, 0] - d[0, 3]) * m0 + jnp.float32(d[0, 1] - d[0, 2]) * m1
+    q1 = jnp.float32(d[1, 0] - d[1, 3]) * m0 + jnp.float32(d[1, 1] - d[1, 2]) * m1
     return [q0 + o0, q1 + o1, q1 - o1, q0 - o0]
 
 
 def slope_x(v):
-    return [slope(v[i]) for i in range(4)]
+    return [slope(v[i], slope_size()) for i in range(4)]
 
 
 def slope_y(v):
-    cols = [slope([v[i][j] for i in range(4)]) for j in range(4)]
+    cols = [slope([v[i][j] for i in range(4)], slope_size()) for j in range(4)]
     return [[cols[j][i] for j in range(4)] for i in range(4)]
 
 
@@ -582,8 +587,80 @@
             v[i][3] = b + jnp.where(ec1 & x_hi, q, next_col(a))
         return v
 
+    ahead_of = jnp.where(er0, lx, ly)
+    starts = ec0 & (ahead_of == 0)
+    ends = ec1 & (ahead_of == last)
+    before_at = jnp.where(starts, source_at, source_at - jnp.where(ec0, step_at, 0))
+    after_at = jnp.where(ends, source_at, source_at + jnp.where(ec1, step_at, 0))
+    up_lane, down_lane = jnp.where(er1, blocks, 0), jnp.where(er0, blocks, 0)
+    right_lane, left_lane = jnp.where(ec1, 1, 0), jnp.where(ec0, 1, 0)
+
+    def inside(at):
+        return jnp.minimum(jnp.maximum(at, 0), LANES - 1)
+
+    corner_at = (
+        (inside(lane - down_lane - left_lane), inside(lane - down_lane + right_lane)),
+        (inside(lane + up_lane - left_lane), inside(lane + up_lane + right_lane)),
+    )
+
+    def flip_col(v):
+        return jnp.where(ec0, up(v, 2, 0), down(v, 2, 0))
+
+    def rims_once(v):
+        flats, talls = [], []
+        for b in range(4):
+            flat = jnp.where(y_hi, v[3][b], v[0][b])
+            flats.append(jnp.where(er0 == y_hi, down(flat, 4, 0), flat))
+            tall = jnp.where(x_hi, v[b][3], v[b][0])
+            tall = jnp.where(ec0 == x_hi, jnp.where(x_hi, up(tall, 2, 0), down(tall, 2, 0)), tall)
+            talls.append(jnp.where(er == ec, tall, down(tall, 4, 0)))
+
+        def found(flat, tall, at):
+            return jnp.where(from_flat, pick(flat, at), pick(tall, at))
+
+        here = [found(flats[b], talls[b], source_at) for b in range(4)]
+        partner = [jnp.where(flipped, flip_col(here[3 - b]), here[b]) for b in range(4)]
+        turned = [(flip_col(flats[b]), flip_col(talls[b])) for b in range(4)]
+        before = jnp.where(flipped, found(flats[0], talls[0], before_at), found(*turned[3], before_at))
+        after = jnp.where(flipped, found(flats[3], talls[3], after_at), found(*turned[0], after_at))
+        return partner + [jnp.where(starts, zero, before), jnp.where(ends, zero, after)]
+
+    def glue_once(v, partner):
+        x00, x03, x30, x33 = v[0][0], v[0][3], v[3][0], v[3][3]
+        before, after = partner[4:]
+        high = er1 & y_hi
+
+        def diagonal(a, n, m):
+            return pick(flip_col(down(a, 4, 0)), corner_at[n][m])
+
+        corners = (
+            (jnp.where(edge_at[0], before, diagonal(x33, 0, 0)), jnp.where(edge_at[0], after, diagonal(x30, 0, 1))),
+            (
+                jnp.where(high, down(before, 4, 0), diagonal(x03, 1, 0)),
+                jnp.where(high, down(after, 4, 0), diagonal(x00, 1, 1)),
+            ),
+        )
+        cols = [(prev_col(row[3]), next_col(row[0])) for row in v]
+        rows = [(prev_row(v[3][j]), next_row(v[0][j])) for j in range(4)]
+        v = [list(row) for row in v]
+        sums = [partner[0] + before, partner[1], partner[2], partner[3] + after]
+        for j in range(4):
+            p = partner[j]
+            v[0][j] = v[0][j] + jnp.where(edge_at[0], p, rows[j][0])
+            v[3][j] = v[3][j] + jnp.where(high, down(p, 4, 0), rows[j][1])
+        for i in range(4):
+            p = sums[i]
+            q = jnp.where(er1, p, down(p, 4, 0))
+            q = jnp.where(er == ec, q, jnp.where(er0, down(q, 2, 0), up(q, 2, 0)))
+            left, right = cols[i]
+            if i in (0, 3):
+                left, right = left + corners[i // 3][0], right + corners[i // 3][1]
+            v[i][0] = v[i][0] + jnp.where(ec0 & x_lo, q, left)
+            v[i][3] = v[i][3] + jnp.where(ec1 & x_hi, q, right)
+        return v
+
     def assemble_one(v):
-        return glue(v, rims(v))
+        return glue_once(v, rims_once(v))
 
     def assemble_pair(u, v):
         pu, pv = rims(u), rims(v)
@@ -692,21 +769,23 @@
         both = receive(got_geo, range(p, pairs, 2))
         put(coef, 2 * p, each(lambda v: jnp.where(lev == 0, v, down(v, 1, 0)), both))
         put(coef, 2 * p + 1, each(lambda v: jnp.where(lev == 1, v, up(v, 1, 0)), both))
-    put(coef, 3, each(lambda v: 1.0 / v, assemble_one(take(coef, 3))))
+    inverse = each(lambda v: 1.0 / v, assemble_one(take(coef, 3)))
+    put(coef, 3, inverse)
+    unit = [[jnp.float32(slope_size() ** 2 * weights[i] * weights[j]) for j in range(4)] for i in range(4)]
+    put(coef, 4, [[unit[i][j] * inverse[i][j] for j in range(4)] for i in range(4)])
 
     def fields_in(k):
         return receive(got, range(k * faces, (k + 1) * faces))
 
-    def scaled(v):
-        return each(lambda a, b: a * b, v, take(coef, 3))
+    def scaled(v, by=4):
+        return each(lambda a, b: a * b, v, take(coef, by))
 
     def laplace_of(v):
         a, b, c = take(coef, 0), take(coef, 1), take(coef, 2)
         gx, gy = slope_x(v), slope_y(v)
         fx = each(lambda p, q, m, n: m * p + n * q, gx, gy, a, b)
         fy = each(lambda p, q, m, n: m * p + n * q, gx, gy, b, c)
-        total = each(lambda p, q: p + q, slope_x(fx), slope_y(fy))
-        return [[jnp.float32(weights[i] * weights[j]) * total[i][j] for j in range(4)] for i in range(4)]
+        return each(lambda p, q: p + q, slope_x(fx), slope_y(fy))
 
     def finish(k, v):
         done = each(lambda s, a: s - hyper_coeff * a, take(section, k), v)
@@ -730,7 +809,7 @@
         return all_of(got, sem_s_in.at[n], sem_r_in.at[n], first, planes)
 
     arrived(0).wait_recv()
-    heat = scaled(assemble_one(fields_in(2)))
+    heat = scaled(assemble_one(fields_in(2)), 3)
     put(section, 2, heat)
     heat = scaled(assemble_one(laplace_of(heat)))
     heat = scaled(assemble_one(laplace_of(heat)))
@@ -739,8 +818,8 @@
     kept(0).start()
     arrived(1).wait_recv()
     wind_u, wind_v = assemble_pair(fields_in(0), fields_in(1))
-    put(section, 0, scaled(wind_u))
-    put(section, 1, scaled(wind_v))
+    put(section, 0, scaled(wind_u, 3))
+    put(section, 1, scaled(wind_v, 3))
     wind_u, wind_v = assemble_pair(laplace_of(take(section, 0)), laplace_of(take(section, 1)))
     wind_u, wind_v = assemble_pair(laplace_of(scaled(wind_u)), laplace_of(scaled(wind_v)))
     finish(0, scaled(wind_u))
@@ -810,7 +889,7 @@
             pltpu.VMEM((SIDE, LANES), jnp.float32),
             pltpu.VMEM(piece, jnp.float32),
             pltpu.VMEM((2 * faces, count, LANES), jnp.float32),
-            pltpu.VMEM((4,) + cells, jnp.float32),
+            pltpu.VMEM((5,) + cells, jnp.float32),
             pltpu.VMEM((3,) + cells, jnp.float32),
             pltpu.VMEM(piece, jnp.float32),
         ]

time: 20.1 us -> 20.1 us (level)
  no operation moved by 1% of the time
where the time goes in v3:
time: 20.1 us; the launch traced here: 20 us
  Pallas kernels  19.9 us (99%)
    pallas_call x1, Pallas kernels, by_level(): pl.pallas_call(functools.partial(main_kernel, groups, blocks), out_shape=...  19.1 us
    pallas_call x1, Pallas kernels, by_level(): pl.pallas_call(last_kernel, out_shape=jax.ShapeDtypeStruct(state.shape, j...  0.86 us

profile of v3, /device:TPU:0, one launch (start us, length us, event | category | flops | bytes accessed | tf_op | source)
XLA Modules:
  0.0 20.0 jit_solution(256700933698430945)
XLA Ops:
  0.0 19.1 %shard_map.73.got = f32[9,32,128]{2,1,0:T(8,128)S(1)} custom-call(s32[4,6]{1,0:T(4,128)} %bitcast.2, s32[4,6]{1,0:T(4,128)} %bitcast.3, f32[3,8,8,192]{3,2,1,0:T(8,128)} %state_in.1, f32[3,8,8]{2,1,0:T(8,128)} %jac_in.1, f32[2,3,8,8]{3,2,1,0:T(8,128)} %diag_in.1, f32[3,8,8]{2,1,0:T(8,128)} %cross_in.1, f32[3,8,8]{2,1,0:T(8,128)} %coriolis_in.1), custom_call_target="tpu_custom_call" | custom-call | tf_op jit(solution)/shard_map/pallas_call | solution.py:879
  19.1 0.9 %shard_map.74 = f32[3,8,8,192]{3,2,1,0:T(8,128)} custom-call(f32[9,32,128]{2,1,0:T(8,128)S(1)} %shard_map.73.got), custom_call_target="tpu_custom_call" | custom-call | tf_op jit(solution)/shard_map/pallas_call | solution.py:899

commit v4 on v2

--- a/solution.py
+++ b/solution.py
@@ -767,22 +767,26 @@
     lane = lax.broadcasted_iota(jnp.int32, (SIDE, LANES), 1)
     first = (lane // 32) % 2 == 0
 
+    widths = 2 * HALF, HALF
+
     def half_rows(n, f, r, h):
         start = (r % 4) * 32 + (r // 4) * 4 + h
-        return jnp.concatenate([mix[n, f, pl.ds(start + ec * 2, 4, stride=8), :] for ec in range(2)], axis=0)
+        return jnp.concatenate([mix[n, f, pl.ds(start + ec * 2, 4, stride=8), 0 : widths[n]] for ec in range(2)], axis=0)
 
     def copy_of(f):
         return pltpu.make_async_copy(full.at[f], out.at[f], sem.at[f])
 
     for f in range(faces):
         u, v, t = (got[k * faces + f] for k in range(3))
-        for m, parts in enumerate(((u, u, v, v), (t, t, t, t))):
-            mix[m, f] = jnp.concatenate(parts, axis=0).T
+        for m, parts in enumerate(((u, u, v, v), (t, t))):
+            mix[m, f, :, 0 : widths[m]] = jnp.concatenate(parts, axis=0).T
     for f in range(faces):
         for r in range(SIDE):
-            wind, temp = (jnp.where(first, half_rows(m, f, r, 0), half_rows(m, f, r, 1)) for m in range(2))
+            wind, temp = (
+                jnp.where(first[:, 0 : widths[m]], half_rows(m, f, r, 0), half_rows(m, f, r, 1)) for m in range(2)
+            )
             full[f, r, :, 0 : 2 * HALF] = wind
-            full[f, r, :, 2 * HALF : 3 * HALF] = temp[:, 0:HALF]
+            full[f, r, :, 2 * HALF : 3 * HALF] = temp
         copy_of(f).start()
     for f in range(faces):
         copy_of(f).wait()

time: 20.1 us -> 20.1 us (level)
  no operation moved by 1% of the time
where the time goes in v4:
time: 20.1 us; the launch traced here: 20 us
  Pallas kernels  20 us (100%)
    pallas_call x1, Pallas kernels, by_level(): pl.pallas_call(functools.partial(main_kernel, groups, blocks), out_shape=...  19.1 us
    pallas_call x1, Pallas kernels, by_level(): pl.pallas_call(last_kernel, out_shape=jax.ShapeDtypeStruct(state.shape, j...  0.86 us

profile of v4, /device:TPU:0, one launch (start us, length us, event | category | flops | bytes accessed | tf_op | source)
XLA Modules:
  0.0 20.0 jit_solution(4211105354410114445)
XLA Ops:
  0.0 19.1 %shard_map.73.got = f32[9,32,128]{2,1,0:T(8,128)S(1)} custom-call(s32[4,6]{1,0:T(4,128)} %bitcast.2, s32[4,6]{1,0:T(4,128)} %bitcast.3, f32[3,8,8,192]{3,2,1,0:T(8,128)} %state_in.1, f32[3,8,8]{2,1,0:T(8,128)} %jac_in.1, f32[2,3,8,8]{3,2,1,0:T(8,128)} %diag_in.1, f32[3,8,8]{2,1,0:T(8,128)} %cross_in.1, f32[3,8,8]{2,1,0:T(8,128)} %coriolis_in.1), custom_call_target="tpu_custom_call" | custom-call | tf_op jit(solution)/shard_map/pallas_call | solution.py:804
  19.1 0.9 %shard_map.74 = f32[3,8,8,192]{3,2,1,0:T(8,128)} custom-call(f32[9,32,128]{2,1,0:T(8,128)S(1)} %shard_map.73.got), custom_call_target="tpu_custom_call" | custom-call | tf_op jit(solution)/shard_map/pallas_call | solution.py:824
